TPU v7x, 32 devices: a whole 2x2x4 slice. The times are simulated.
32 devices in a mesh: pop: 16 (over z, y, core), fsdp: 2 (over x).
Axes of the slice: x: 2, y: 2, z: 4, core: 2. Of those that a mesh axis runs over, the one named last changes fastest.
Arguments:
- tokens: bfloat16 [14336, 4096], P('pop', 'fsdp'), may hold values from -6 to 6
- up_weight: bfloat16 [4096, 14336], P('pop', 'fsdp'), may hold values from -0.09375 to 0.09375
- a_bank: bfloat16 [1024, 4096], P(None, 'pop'), may hold values from -6 to 6
- b_bank: bfloat16 [1024, 14336], P(None, 'fsdp'), may hold values from -6 to 6
- factor_index: int32 [32, 4], replicated, may hold values from 0 to 1023
- mirror: int32 [32], P('pop'), may hold values 0 or 1
- rewards: int32 [32], P('pop'), may hold values from -8 to 7
Outputs:
- hidden: bfloat16 [14336, 14336], P('pop', 'fsdp')
- update: float32 [4096, 14336], P('pop', 'fsdp')
All inputs are finite; a program needn't handle non-finite values. No bound on the sum of `mirror` on one device may be relied on, other than what follows from the above.
Results may differ from a plain program's by a relative error of at most 0.001.
Values may be sent and summed in bfloat16 or wider, within the bound.
No kernel may reach another device: no remote copies, remote signals or barrier semaphores. Data moves between devices by JAX's collectives and lax.ppermute only.
A program may use at most 192 MiB of HBM per device.

v0:
```python
import math

import jax
import jax.numpy as jnp
from jax import lax
from jax.sharding import PartitionSpec as P

D = 4096
RANK = 4
SEQ = 448


noise_scale = 0.5


def shaped_weights(rewards, mirror):
    members_all = rewards.shape[0]
    member_ids = jnp.arange(members_all)
    beaten = rewards[None, :] < rewards[:, None]
    level_tie = (rewards[None, :] == rewards[:, None]) & (member_ids[None, :] < member_ids[:, None])
    standing = jnp.sum((beaten | level_tie).astype(jnp.int32), axis=1)
    signed = (2 * mirror - 1).astype(jnp.float32)
    shaped = 2.0 * standing.astype(jnp.float32) / (members_all - 1) - 1.0
    return shaped * signed / math.sqrt(members_all * RANK)


def per_device(tokens, up_weight, a_bank, b_bank, factor_index, mirror, rewards):
    members_here = mirror.shape[0]
    own_width = members_here * RANK
    position = lax.axis_index("pop")
    flat_index = factor_index.reshape(-1)
    picked_a = jnp.take(a_bank, flat_index, axis=0)
    picked_b = jnp.take(b_bank, flat_index, axis=0)
    first_own = position * own_width
    gathered_a, rewards_all, mirror_all = (
        lax.all_gather(picked_a, "pop", axis=1, tiled=True),
        lax.all_gather(rewards, "pop", axis=0, tiled=True),
        lax.all_gather(mirror, "pop", axis=0, tiled=True),
    )
    own_a = lax.dynamic_slice_in_dim(gathered_a, first_own, own_width, 0)
    own_b = lax.dynamic_slice_in_dim(picked_b, first_own, own_width, 0).astype(jnp.float32)
    own_signs = (2 * mirror - 1).astype(jnp.float32)
    column_factor = jnp.repeat(noise_scale / math.sqrt(D * RANK) * own_signs, RANK)
    member_of_column = jnp.arange(own_width) // RANK
    row_count = tokens.shape[0]
    entire_weight = lax.all_gather(up_weight, "pop", axis=0, tiled=True)
    piece = lax.all_gather(tokens, "fsdp", axis=1, tiled=True)
    dense_sum = jnp.dot(piece, entire_weight, preferred_element_type=jnp.float32)
    low_sum = jnp.dot(piece, own_a.T, preferred_element_type=jnp.float32)
    member_of_row = jnp.arange(row_count) // SEQ
    same_member = member_of_row[:, None] == member_of_column[None, :]
    scaled = jnp.where(same_member, low_sum * column_factor[None, :], 0.0)
    perturbed = jnp.dot(scaled, own_b, precision=lax.Precision.HIGHEST)
    hidden = (dense_sum + perturbed).astype(jnp.bfloat16)
    weighting = shaped_weights(rewards_all, mirror_all)
    spread = jnp.repeat(weighting, RANK)
    update = jnp.dot(
        picked_a.astype(jnp.float32).T,
        spread[:, None] * picked_b.astype(jnp.float32),
        precision=lax.Precision.HIGHEST,
    )
    return (hidden, update)


def solution(mesh):
    in_specs = (
        P("pop", "fsdp"),
        P("pop", "fsdp"),
        P(None, "pop"),
        P(None, "fsdp"),
        P(),
        P("pop"),
        P("pop"),
    )
    out_specs = (P("pop", "fsdp"), P("pop", "fsdp"))
    return jax.shard_map(
        per_device, mesh=mesh, in_specs=in_specs, out_specs=out_specs, check_vma=False
    )
```

profile of v0, /device:TPU:0, one launch (start us, length us, event | category | flops | bytes accessed | tf_op | source)
XLA Modules:
  0.0 500.3 jit_solution(14490120809705713757)
XLA Ops:
  7.2 0.8 copy.13
  8.0 0.1 reshape.74
  8.2 0.1 reshape.73
  8.3 0.8 gather_fusion
  9.2 0.7 broadcast_select_fusion.1
  9.9 0.7 all-gather.4.cloned.1.call-update
  10.7 0.7 all-gather.6.cloned.1.call-update
  11.5 0.1 mul.46
  11.6 11.7 %gather_fusion.1 = bf16[128,7168]{1,0:T(8,128)(2,1)} fusion(bf16[1024,7168]{1,0:T(8,128)(2,1)} %param.10, s32[1024]{0:T(1024)S(1)} %pad_clamp_fusion), kind=kCustom, calls=%fused_computation.1 | custom fusion | bytes 3670528 | tf_op jit(solution)/shard_map/jit(_take)/gather | solution.py:33
  23.3 0.6 dynamic-slice
  24.5 0.2 dynamic-update-slice.1
  24.7 0.2 dynamic-update-slice
  25.0 13.8 %all-reduce.2 = (s32[32]{0:T(128)S(1)}, s32[32]{0:T(128)S(1)}) all-reduce(s32[32]{0:T(128)S(1)} %dynamic-update-slice.1, s32[32]{0:T(128)S(1)} %dynamic-update-slice), channel_id=1, replica_groups=mesh['pop'=16,'fsdp'=2] {'pop'}, use_global_device_ids=true, to_apply=%add.1 | all-reduce | flops 64 | bytes 512
  38.7 0.2 convert_reduce_fusion
  38.9 0.1 broadcast_in_dim.44
  39.0 0.1 mul.53
  39.1 1.7 broadcast_select_fusion
  40.9 5.3 %fusion = f32[256,7168]{1,0:T(8,128)} fusion(bf16[128,256]{1,0:T(8,128)(2,1)S(1)} %copy-done.2, bf16[128,7168]{1,0:T(8,128)(2,1)S(1)} %broadcast_select_fusion, f32[128]{0:T(128)S(1)} %mul.53), kind=kOutput, calls=%fused_computation.3 | convolution fusion | flops 2820407296 | bytes 9241088 | tf_op jit(solution)/shard_map/dot_general | solution.py:57
  46.2 3.9 all-gather.8.cloned.1.call-done
  50.1 93.3 %all-gather.4.cloned.1.call-done = bf16[896,4096]{1,0:T(8,128)(2,1)} async-done(((bf16[896,2048]{1,0:T(8,128)(2,1)}), bf16[896,4096]{1,0:T(8,128)(2,1)}) %all-gather.4.cloned.1.call-update) | async-done | bytes 7340048 | tf_op jit(solution)/shard_map/all_gather | solution.py:47
  143.5 5.1 %fusion.5 = f32[896,8]{0,1:T(8,128)S(1)} fusion(bf16[896,4096]{1,0:T(8,128)(2,1)} %all-gather.4.cloned.1.call-done, bf16[128,4096]{1,0:T(8,128)(2,1)} %all-gather.8.cloned.1.call-done, s32[]{:T(128)S(6)} %select_n.57, f32[8]{0:T(128)S(1)} %mul.46, s32[896]{0:T(1024)S(1)} %add_select_fusion, s32[8]{0:T(128)S(1)} %and_select_fusion), kind=kOutput, calls=%fused_computation.10 | convolution fusion | flops 58741760 | bytes 7437892 | tf_op jit(solution)/shard_map/dot_general | solution.py:49
  148.6 14.9 %fusion.6 = f32[896,7168]{1,0:T(8,128)} fusion(f32[896,8]{0,1:T(8,128)S(1)} %fusion.5, bf16[128,7168]{1,0:T(8,128)(2,1)S(1)} %broadcast_select_fusion, s32[]{:T(128)S(6)} %select_n.57), kind=kOutput, calls=%fused_computation.11 | convolution fusion | flops 616562688 | bytes 25833476 | tf_op jit(solution)/shard_map/dot_general | solution.py:53
  163.5 268.2 %all-gather.6.cloned.1.call-done = bf16[4096,7168]{1,0:T(8,128)(2,1)} async-done(((bf16[256,7168]{1,0:T(8,128)(2,1)}), bf16[4096,7168]{1,0:T(8,128)(2,1)}) %all-gather.6.cloned.1.call-update) | async-done | bytes 58720272 | tf_op jit(solution)/shard_map/all_gather | solution.py:46
  431.7 62.0 %add_convert_fusion = bf16[896,7168]{1,0:T(8,128)(2,1)} fusion(f32[896,7168]{1,0:T(8,128)} %fusion.6, bf16[896,4096]{1,0:T(8,128)(2,1)} %all-gather.4.cloned.1.call-done, bf16[4096,7168]{1,0:T(8,128)(2,1)} %all-gather.6.cloned.1.call-done), kind=kOutput, calls=%fused_computation.2 | convolution fusion | flops 52626194432 | bytes 104595456 | tf_op jit(solution)/shard_map/dot_general | solution.py:48
  (26 shorter events, 0.3 us)
Async XLA Ops:
  7.2 1.1 copy-start
  7.2 4.2 copy-start.3
  7.2 42.9 %all-gather.8.cloned.1.call-start = ((), (), s32[]{:S(2)}) async-start(), calls=%async_computation.2 | async-start | bytes 1114112 | tf_op jit(solution)/shard_map/all_gather | solution.py:36
  9.9 133.6 %all-gather.4.cloned.1.call-start = ((), (), s32[]{:S(2)}) async-start(), calls=%async_computation | async-start | bytes 11010048 | tf_op jit(solution)/shard_map/all_gather | solution.py:47
  10.7 421.0 %all-gather.6.cloned.1.call-start = ((), (), s32[]{:S(2)}) async-start(), calls=%async_computation.1 | async-start | bytes 62390272 | tf_op jit(solution)/shard_map/all_gather | solution.py:46
  11.6 11.7 %copy-start.5 = (u32[32]{0:T(128)S(1)}, u32[32]{0:T(128)}, u32[]{:S(2)}) copy-start(u32[32]{0:T(128)} %constant.89) | copy-start | bytes 388
  11.6 13.2 %copy-start.4 = (s32[2]{0:T(128)S(1)}, s32[2]{0:T(128)}, u32[]{:S(2)}) copy-start(s32[2]{0:T(128)} %param.13) | copy-start | bytes 28
  11.6 29.3 %copy-start.2 = (bf16[128,256]{1,0:T(8,128)(2,1)S(1)}, bf16[128,256]{1,0:T(8,128)(2,1)}, u32[]{:S(2)}) copy-start(bf16[128,256]{1,0:T(8,128)(2,1)} %broadcast_select_fusion.1) | copy-start | bytes 196612
  431.7 62.0 %copy-start.1 = (bf16[1024,256]{1,0:T(8,128)(2,1)S(1)}, bf16[1024,256]{1,0:T(8,128)(2,1)}, u32[]{:S(2)}) copy-start(bf16[1024,256]{1,0:T(8,128)(2,1)} %param.9) | copy-start | bytes 1572868
Sparse Core Ops, SparseCore 0:
  10.7 39.3 all-gather.7
  51.7 91.7 all-gather.3
  145.1 286.5 all-gather.5
where the time goes:
time: 500 us
  waiting for transfers between devices  367 us (73%)
  matrix products  87.4 us (17%)
  local copies, waits for them, and re-layouts  15 us (3%)
  between operations  14.5 us (3%)
  blocking collectives  13.8 us (3%)
    all_gather x1, waiting for transfers between devices, per_device(): entire_weight = lax.all_gather(up_weight, 'pop', axis=0, tiled=True)  268 us
    all_gather x1, waiting for transfers between devices, per_device(): piece = lax.all_gather(tokens, 'fsdp', axis=1, tiled=True)  93.3 us
    dot_general x1, matrix products, per_device(): jnp.dot(piece, entire_weight, preferred_element_type=jnp.float32)  62 us
    dot_general x1, matrix products, per_device(): perturbed = jnp.dot(scaled, own_b, precision=lax.Precision.HIGHEST)  14.9 us
    unnamed x1, blocking collectives  13.8 us
    gather x1, local copies, waits for them, and re-layouts, per_device(): picked_b = jnp.take(b_bank, flat_index, axis=0)  11.7 us
  transfers between devices with their start and end apart: 3, of which 3 were waited for; matrix products, arithmetic and copies ran while one was open for 8% of the time, Pallas kernels for 0%

commit v1 on v0

v1 whole, which is shorter than its diff:
```python
import math

import jax
import jax.numpy as jnp
from jax import lax
from jax.experimental import pallas as pl
from jax.experimental.pallas import tpu as pltpu
from jax.sharding import PartitionSpec as P


D = 4096
RANK = 4
SEQ = 448
LANES = 128
LATE_SHARE = 7


noise_scale = 0.5


def shaped_weights(rewards, mirror):
    members_all = rewards.shape[0]
    member_ids = jnp.arange(members_all)
    beaten = rewards[None, :] < rewards[:, None]
    level_tie = (rewards[None, :] == rewards[:, None]) & (member_ids[None, :] < member_ids[:, None])
    standing = jnp.sum((beaten | level_tie).astype(jnp.int32), axis=1)
    signed = (2 * mirror - 1).astype(jnp.float32)
    shaped = 2.0 * standing.astype(jnp.float32) / (members_all - 1) - 1.0
    return shaped * signed / math.sqrt(members_all * RANK)


def whole_rows(tokens, parts):
    me = lax.axis_index("fsdp")
    width = tokens.shape[1]
    full = jnp.zeros((tokens.shape[0], width * parts), tokens.dtype)
    full = lax.dynamic_update_slice_in_dim(full, tokens, me * width, 1)
    for shift in range(1, parts):
        ring = [(i, (i + shift) % parts) for i in range(parts)]
        arrived = lax.ppermute(tokens, "fsdp", ring)
        owner = (me - shift + parts) % parts
        full = lax.dynamic_update_slice_in_dim(full, arrived, owner * width, 1)
    return full


def projection_kernel(x_ref, low_ref, w_ref, b_ref, *rest):
    out_ref = rest[-1]
    total = jnp.dot(x_ref[...], w_ref[...], preferred_element_type=jnp.float32)
    total += jnp.dot(low_ref[...], b_ref[...], preferred_element_type=jnp.float32)
    out_ref[...] = total.astype(out_ref.dtype)


def project(x, low_terms, weight, b_terms, start, into=None):
    rows, depth = x.shape
    width, columns = weight.shape[1], b_terms.shape[1]
    block = next(size for size in (512, 256, LANES) if width % size == 0 and start % size == 0)
    if into is not None:
        block = min(block, 2 * LANES)
    first = start // block
    operands = [x, low_terms, weight, b_terms]
    in_specs = [
        pl.BlockSpec(memory_space=pltpu.VMEM),
        pl.BlockSpec(memory_space=pltpu.VMEM),
        pl.BlockSpec((depth, block), lambda i: (0, i)),
        pl.BlockSpec((b_terms.shape[0], block), lambda i: (0, first + i)),
    ]
    aliases = {}
    if into is not None:
        operands.append(into)
        in_specs.append(pl.BlockSpec(memory_space=pl.ANY))
        aliases = {4: 0}
    return pl.pallas_call(
        projection_kernel,
        grid=(width // block,),
        in_specs=in_specs,
        out_specs=pl.BlockSpec((rows, block), lambda i: (0, first + i)),
        out_shape=jax.ShapeDtypeStruct((rows, columns), jnp.bfloat16),
        input_output_aliases=aliases,
        cost_estimate=pl.CostEstimate(
            flops=2 * rows * depth * width,
            bytes_accessed=2 * (depth * width + rows * width),
            transcendentals=0,
        ),
        compiler_params=pltpu.CompilerParams(
            vmem_limit_bytes=40 * 1024 * 1024, dimension_semantics=("arbitrary",)
        ),
    )(*operands)


def three_terms(value):
    terms = []
    for _ in range(3):
        term = lax.reduce_precision(value, 8, 7)
        terms.append(term.astype(jnp.bfloat16))
        value = value - term
    return jnp.concatenate(terms, axis=1)


def per_device(parts, tokens, up_weight, a_bank, b_bank, factor_index, mirror, rewards):
    members_here = mirror.shape[0]
    own_width = members_here * RANK
    position = lax.axis_index("pop")
    flat_index = factor_index.reshape(-1)
    columns = up_weight.shape[1]
    late = max(1, columns // LANES // LATE_SHARE) * LANES
    early = columns - late
    weight_early = lax.all_gather(up_weight[:, :early], "pop", axis=0, tiled=True)
    weight_late = lax.all_gather(up_weight[:, early:], "pop", axis=0, tiled=True)
    piece = whole_rows(tokens, parts)

    picked_a = jnp.take(a_bank, flat_index, axis=0)
    picked_b = jnp.take(b_bank, flat_index, axis=0)
    first_own = position * own_width
    own_a = lax.all_to_all(picked_a, "pop", split_axis=0, concat_axis=1, tiled=True)
    rewards_all, mirror_all = (
        lax.all_gather(rewards, "pop", axis=0, tiled=True),
        lax.all_gather(mirror, "pop", axis=0, tiled=True),
    )
    own_b = lax.dynamic_slice_in_dim(picked_b, first_own, own_width, 0)
    own_signs = (2 * mirror - 1).astype(jnp.float32)
    column_factor = jnp.repeat(noise_scale / math.sqrt(D * RANK) * own_signs, RANK)
    member_of_column = jnp.arange(own_width) // RANK
    row_count = tokens.shape[0]
    low_sum = jnp.dot(piece, own_a.T, preferred_element_type=jnp.float32)
    member_of_row = jnp.arange(row_count) // SEQ
    same_member = member_of_row[:, None] == member_of_column[None, :]
    scaled = jnp.where(same_member, low_sum * column_factor[None, :], 0.0)
    low_terms = three_terms(scaled)
    b_terms = jnp.concatenate([own_b] * 3, axis=0)

    weighting = shaped_weights(rewards_all, mirror_all)
    spread = jnp.repeat(weighting, RANK)
    update = jnp.dot(
        picked_a.astype(jnp.float32).T,
        spread[:, None] * picked_b.astype(jnp.float32),
        precision=lax.Precision.HIGHEST,
    )

    hidden = project(piece, low_terms, weight_early, b_terms, 0)
    hidden = project(piece, low_terms, weight_late, b_terms, early, hidden)
    return (hidden, update)


def solution(mesh):
    parts = mesh.shape["fsdp"]

    def body(*args):
        return per_device(parts, *args)

    in_specs = (
        P("pop", "fsdp"),
        P("pop", "fsdp"),
        P(None, "pop"),
        P(None, "fsdp"),
        P(),
        P("pop"),
        P("pop"),
    )
    out_specs = (P("pop", "fsdp"), P("pop", "fsdp"))
    return jax.shard_map(
        body, mesh=mesh, in_specs=in_specs, out_specs=out_specs, check_vma=False
    )
```

time: 500 us -> 359 us (0.72)
  waiting for transfers between devices: 367 us -> 211 us
  matrix products: 87.4 us -> 10.9 us
  Pallas kernels: 0 us -> 68.6 us
  local copies, waits for them, and re-layouts: 15 us -> 30 us
  starting transfers between devices: 0.12 us -> 9.05 us
    all_gather x3 -> x2, waiting for transfers between devices: 365 us -> 177 us  [the longest x1 156 us: per_device(): lax.all_gather(up_weight[:, :early], 'pop', axis=0, tiled=True)]
    dot_general x2 -> x0, matrix products: 76.9 us -> none  [the longest x1 62 us: per_device(): jnp.dot(piece, entire_weight, preferred_element_type=jnp.float32)]
    pallas_call x0 -> x2, Pallas kernels: none -> 68.6 us  [project(): pl.pallas_call(projection_kernel, grid=(width // block,), in_specs=in_spe...]
    ppermute x0 -> x1, waiting for transfers between devices: none -> 33.8 us  [whole_rows(): arrived = lax.ppermute(tokens, 'fsdp', ring)]
    dynamic_update_slice x0 -> x2, local copies, waits for them, and re-layouts: none -> 6.87 us  [the longest x1 4.47 us: whole_rows(): full = lax.dynamic_update_slice_in_dim(full, arrived, owner * width, 1)]
    all_to_all x0 -> x1, starting transfers between devices: none -> 5.94 us  [per_device(): lax.all_to_all(picked_a, 'pop', split_axis=0, concat_axis=1, tiled=True)]
    slice x0 -> x2, local copies, waits for them, and re-layouts: none -> 5.8 us  [the longest x1 3.93 us: per_device(): up_weight[:, :early]]
  transfers between devices with their start and end apart: 3 -> 4, of which waited for: 3 -> 3; matrix products, arithmetic and copies ran while one was open for 8% -> 11% of each run, Pallas kernels for 0% -> 15%
where the time goes in v1:
time: 359 us
  waiting for transfers between devices  211 us (59%)
  Pallas kernels  68.6 us (19%)
  local copies, waits for them, and re-layouts  30 us (8%)
  between operations  14.9 us (4%)
  blocking collectives  13 us (4%)
  matrix products  10.9 us (3%)
  starting transfers between devices  9.05 us (3%)
    all_gather x1, waiting for transfers between devices, per_device(): lax.all_gather(up_weight[:, :early], 'pop', axis=0, tiled=True)  156 us
    pallas_call x2, Pallas kernels, project(): pl.pallas_call(projection_kernel, grid=(width // block,), in_specs=in_spe...  68.6 us
    ppermute x1, waiting for transfers between devices, whole_rows(): arrived = lax.ppermute(tokens, 'fsdp', ring)  33.8 us
    all_gather x1, waiting for transfers between devices, per_device(): lax.all_gather(up_weight[:, early:], 'pop', axis=0, tiled=True)  21.1 us
    unnamed x1, blocking collectives  13 us
    gather x1, local copies, waits for them, and re-layouts, per_device(): picked_b = jnp.take(b_bank, flat_index, axis=0)  10.5 us
  transfers between devices with their start and end apart: 4, of which 3 were waited for; matrix products, arithmetic and copies ran while one was open for 11% of the time, Pallas kernels for 15%

profile of v1, /device:TPU:0, one launch (start us, length us, event | category | flops | bytes accessed | tf_op | source)
XLA Modules:
  0.0 358.9 jit_solution(9051019306426169001)
XLA Ops:
  7.2 3.9 %slice.7 = bf16[256,6144]{1,0:T(8,128)(2,1)} slice(bf16[256,7168]{1,0:T(8,128)(2,1)} %param.8), slice={[0:256], [0:6144]} | slice | bytes 6291456 | tf_op jit(solution)/shard_map/slice | solution.py:106
  11.2 1.9 slice.6
  13.1 3.0 collective-permute-start
  16.5 0.8 gather_fusion
  17.3 0.7 bitcast_select_fusion
  18.0 5.9 %all-to-all-start = ((bf16[16,8,256]{2,1,0:T(8,128)(2,1)}), bf16[16,8,256]{2,1,0:T(8,128)(2,1)S(1)}, u32[]{:S(2)}, u32[]{:S(2)}) async-start(bf16[16,8,256]{2,1,0:T(8,128)(2,1)} %bitcast_select_fusion), calls=%async_computation | async-start | bytes 131072 | tf_op jit(solution)/shard_map/all_to_all | solution.py:113
  24.3 10.5 %gather_fusion.1 = bf16[128,7168]{1,0:T(8,128)(2,1)S(1)} fusion(bf16[1024,7168]{1,0:T(8,128)(2,1)} %param.10, s32[1024]{0:T(1024)S(1)} %pad_clamp_fusion), kind=kCustom, calls=%fused_computation.1 | custom fusion | bytes 3670528 | tf_op jit(solution)/shard_map/jit(_take)/gather | solution.py:111
  34.8 0.6 dynamic-slice
  36.0 0.2 dynamic-update-slice.1
  36.3 0.2 dynamic-update-slice
  36.5 13.0 %all-reduce.2 = (s32[32]{0:T(128)S(1)}, s32[32]{0:T(128)S(1)}) all-reduce(s32[32]{0:T(128)S(1)} %dynamic-update-slice.1, s32[32]{0:T(128)S(1)} %dynamic-update-slice), channel_id=1, replica_groups=mesh['pop'=16,'fsdp'=2] {'pop'}, use_global_device_ids=true, to_apply=%add.1 | all-reduce | flops 64 | bytes 512
  49.5 0.2 convert_reduce_fusion
  49.9 4.0 %broadcast_in_dim.45 = bf16[896,4096]{1,0:T(8,128)(2,1)} broadcast(bf16[]{:T(256)} %constant.85.clone.1), dimensions={} | broadcast | bytes 7340034 | tf_op jit(solution)/shard_map/broadcast_in_dim | solution.py:35
  53.9 2.4 constant_dynamic-update-slice_fusion.1
  56.3 5.4 %fusion = f32[256,7168]{1,0:T(8,128)} fusion(f32[128]{0:T(128)S(1)} %mul.57, bf16[128,256]{1,0:T(8,128)(2,1)S(1)} %gather_fusion, pred[128]{0:T(512)(128)(4,1)S(1)} %compare_and_fusion.1, bf16[128,7168]{1,0:T(8,128)(2,1)S(1)} %gather_fusion.1), kind=kOutput, calls=%fused_computation.2 | convolution fusion | flops 2821357568 | bytes 9241216 | tf_op jit(solution)/shard_map/dot_general | solution.py:132
  61.8 0.2 broadcast_select_fusion
  62.1 33.8 %collective-permute-done = bf16[896,2048]{1,0:T(8,128)(2,1)} collective-permute-done((bf16[896,2048]{1,0:T(8,128)(2,1)}, bf16[896,2048]{1,0:T(8,128)(2,1)}, u32[]{:S(2)}, u32[]{:S(2)}) %collective-permute-start) | collective-permute-done | bytes 3670048 | tf_op jit(solution)/shard_map/ppermute | solution.py:39
  95.8 4.5 %constant_dynamic-update-slice_fusion.x_ref = bf16[896,4096]{1,0:T(8,128)(2,1)} fusion(bf16[896,4096]{1,0:T(8,128)(2,1)} %constant_dynamic-update-slice_fusion.1, bf16[896,2048]{1,0:T(8,128)(2,1)} %collective-permute-done, s32[]{:T(128)S(6)} %select_n.72), kind=kLoop, calls=%fused_computation.43 | loop fusion | bytes 7340036 | tf_op jit(solution)/shard_map/dynamic_update_slice | solution.py:41
  100.3 5.5 %reduce-precision_convert_fusion.1 = (bf16[896,8]{0,1:T(8,128)(2,1)S(1)}, bf16[896,8]{0,1:T(8,128)(2,1)S(1)}, bf16[896,8]{0,1:T(8,128)(2,1)S(1)}) fusion(f32[8]{0:T(128)S(1)} %mul.50, bf16[896,4096]{1,0:T(8,128)(2,1)} %constant_dynamic-update-slice_fusion.x_ref, bf16[8,4096]{1,0:T(8,128)(2,1)S(1)} %bitcast.10, s32[8]{0:T(128)S(1)} %and_select_fusion, ...), kind=kOutput, calls=%fused_computation.17 | convolution fusion | flops 58799104 | bytes 7452224 | tf_op jit(solution)/shard_map/dot_general | solution.py:123
  105.8 0.2 copy.27.low_ref
  106.0 156.4 %all-gather.5.cloned.1.call-done.w_ref = bf16[4096,6144]{1,0:T(8,128)(2,1)} async-done(((bf16[256,6144]{1,0:T(8,128)(2,1)}), bf16[4096,6144]{1,0:T(8,128)(2,1)}) %all-gather.5.cloned.1.call-update) | async-done | bytes 50331664 | tf_op jit(solution)/shard_map/all_gather | solution.py:106
  262.4 55.3 %shard_map.86.rest_0_ = bf16[896,7168]{1,0:T(8,128)(2,1)} custom-call(bf16[896,4096]{1,0:T(8,128)(2,1)} %constant_dynamic-update-slice_fusion.x_ref, bf16[896,24]{1,0:T(8,128)(2,1)S(1)} %copy.27.low_ref, bf16[4096,6144]{1,0:T(8,128)(2,1)} %all-gather.5.cloned.1.call-done.w_ref, bf16[24,7168]{1,0:T(8,128)(2,1)S(1)} %pad_maximum_fusion.b_ref), custom_call_target="tpu_custom_call" | custom-call | flops 45097156608 | bytes 61341696 | tf_op jit(solution)/shard_map/pallas_call | solution.py:71
  317.7 21.1 %all-gather.3.cloned.1.call-done.w_ref = bf16[4096,1024]{1,0:T(8,128)(2,1)} async-done(((bf16[256,1024]{1,0:T(8,128)(2,1)}), bf16[4096,1024]{1,0:T(8,128)(2,1)}) %all-gather.3.cloned.1.call-update) | async-done | bytes 8388624 | tf_op jit(solution)/shard_map/all_gather | solution.py:107
  338.8 13.2 %shard_map.87 = bf16[896,7168]{1,0:T(8,128)(2,1)} custom-call(bf16[896,4096]{1,0:T(8,128)(2,1)} %constant_dynamic-update-slice_fusion.x_ref, bf16[896,24]{1,0:T(8,128)(2,1)S(1)} %copy.27.low_ref, bf16[4096,1024]{1,0:T(8,128)(2,1)} %all-gather.3.cloned.1.call-done.w_ref, bf16[24,7168]{1,0:T(8,128)(2,1)S(1)} %pad_maximum_fusion.b_ref, ...), custom_call_target="tpu_custom_call", output_to_operand_aliasing={{}: (4, {})} | custom-call | flops 7516192768 | bytes 10223616 | tf_op jit(solution)/shard_map/pallas_call | solution.py:71
  (40 shorter events, 1.0 us)
Async XLA Ops:
  7.2 9.3 %copy-start = (bf16[1024,256]{1,0:T(8,128)(2,1)S(1)}, bf16[1024,256]{1,0:T(8,128)(2,1)}, u32[]{:S(2)}) copy-start(bf16[1024,256]{1,0:T(8,128)(2,1)} %param.9) | copy-start | bytes 1572868
  7.2 255.2 %all-gather.5.cloned.1.call-start = ((), (), s32[]{:S(2)}) async-start(), calls=%async_computation.2 | async-start | bytes 53477376 | tf_op jit(solution)/shard_map/all_gather | solution.py:106
  11.2 5.0 %copy-start.3 = (s32[32,4]{0,1:T(4,128)S(1)}, s32[32,4]{0,1:T(4,128)}, u32[]{:S(2)}) copy-start(s32[32,4]{0,1:T(4,128)} %param.11) | copy-start | bytes 1540
  11.2 12.9 %copy-start.4 = (s32[2]{0:T(128)S(1)}, s32[2]{0:T(128)}, u32[]{:S(2)}) copy-start(s32[2]{0:T(128)} %param.12) | copy-start | bytes 28
  11.2 327.6 %all-gather.3.cloned.1.call-start = ((), (), s32[]{:S(2)}) async-start(), calls=%async_computation.1 | async-start | bytes 8912896 | tf_op jit(solution)/shard_map/all_gather | solution.py:107
  13.1 82.7 %collective-permute-start = (bf16[896,2048]{1,0:T(8,128)(2,1)}, bf16[896,2048]{1,0:T(8,128)(2,1)}, u32[]{:S(2)}, u32[]{:S(2)}) collective-permute-start(bf16[896,2048]{1,0:T(8,128)(2,1)} %param.7), channel_id=1, source_target_pairs={{0,1},{1,0},{2,3},{3,2},{4,5},{5,4},{6,7},{7,6},{8,9},{9,8},{10,11... | collective-permute-start | bytes 11010056 | tf_op jit(solution)/shard_map/ppermute | solution.py:39
  18.0 82.3 %all-to-all-start = ((bf16[16,8,256]{2,1,0:T(8,128)(2,1)}), bf16[16,8,256]{2,1,0:T(8,128)(2,1)S(1)}, u32[]{:S(2)}, u32[]{:S(2)}) async-start(bf16[16,8,256]{2,1,0:T(8,128)(2,1)} %bitcast_select_fusion), calls=%async_computation | async-start | bytes 131072 | tf_op jit(solution)/shard_map/all_to_all | solution.py:113
  24.3 10.5 %copy-start.6 = (u32[32]{0:T(128)S(1)}, u32[32]{0:T(128)}, u32[]{:S(2)}) copy-start(u32[32]{0:T(128)} %constant.110) | copy-start | bytes 388
  24.3 12.0 %copy-start.5 = (s32[2]{0:T(128)S(1)}, s32[2]{0:T(128)}, u32[]{:S(2)}) copy-start(s32[2]{0:T(128)} %param.13) | copy-start | bytes 28
  49.9 4.0 %copy-start.2 = (bf16[896,2048]{1,0:T(8,128)(2,1)S(1)}, bf16[896,2048]{1,0:T(8,128)(2,1)}, u32[]{:S(2)}) copy-start(bf16[896,2048]{1,0:T(8,128)(2,1)} %param.7) | copy-start | bytes 11010052
  338.8 13.2 %copy-start.1 = (bf16[1024,256]{1,0:T(8,128)(2,1)S(1)}, bf16[1024,256]{1,0:T(8,128)(2,1)}, u32[]{:S(2)}) copy-start(bf16[1024,256]{1,0:T(8,128)(2,1)} %param.9) | copy-start | bytes 1572868
Sparse Core Ops, SparseCore 0:
  11.3 251.0 all-gather.4
  264.5 74.2 all-gather.2
